TPU v7x, 32 devices: a whole 2x2x4 slice. The times are simulated.
32 devices in a mesh: ep: 8 (over y, x, core), tp: 4 (over z).
Axes of the slice: x: 2, y: 2, z: 4, core: 2. Of those that a mesh axis runs over, the one named last changes fastest.
Arguments:
- tokens: bfloat16 [256, 4096], P('ep', 'tp'), may hold values from -6 to 6
- norm_gains: float32 [2, 4096], replicated, may hold values from 0.1 to 1.9
- router: bfloat16 [2, 4096, 16], replicated, as said below
- w_gate: bfloat16 [2, 16, 4096, 768], P(None, 'ep', None, 'tp'), may hold values from -0.09375 to 0.09375
- w_up: bfloat16 [2, 16, 4096, 768], P(None, 'ep', None, 'tp'), may hold values from -0.09375 to 0.09375
- w_down: bfloat16 [2, 16, 768, 4096], P(None, 'ep', 'tp'), may hold values from -0.21875 to 0.21875
- expert_ids: int32 [2, 256, 8], P(None, 'ep'), may hold values from 0 to 15, all different within a row; in each aligned block of 32 rows (0 to 31, 32 to 63, ...) at most 32 rows name the same one
Outputs:
- hidden_out: bfloat16 [256, 4096], P('ep', 'tp')
Inputs may be any that keep to these rules, and one draw needn't show every extreme that they name: `expert_ids`: each entry names an expert of 0 to 15; the 8 entries of a token differ; among the 32 tokens of one ep index in one layer no expert is named more than 32 times, and in some such blocks one is named exactly 32 times. `router`: entries of order 2 / sqrt(4096); all columns of a layer may share a common added vector with entries of order 50 / sqrt(4096).
All inputs are finite; a program needn't handle non-finite values.
Results may differ from a plain program's by a relative error of at most 0.02.
Values may be sent and summed in bfloat16 or wider, within the bound.
A program may use at most 64 MiB of HBM per device.

v0:
```python
import jax
import jax.numpy as jnp
from jax import lax
from jax.sharding import PartitionSpec as P

TOP = 8
LAYERS = 2
norm_eps = 1e-06


def body(tokens, norm_gains, router, w_gate, w_up, w_down, expert_ids):
    n_tp = lax.axis_size("tp")
    n_ep = lax.axis_size("ep")
    local_width = tokens.shape[1]
    full_width = local_width * n_tp
    rows_dev = tokens.shape[0]
    local_exp = w_gate.shape[1]
    experts = local_exp * n_ep
    capacity = 2 * rows_dev * TOP // experts
    current = tokens
    for layer_idx in range(LAYERS):
        gain = norm_gains[layer_idx]
        weight = router[layer_idx]
        ids = expert_ids[layer_idx]
        normed = None
        whole = lax.all_gather(current, "tp", axis=1, tiled=True)
        wide_rows = whole.astype(jnp.float32)
        square_sum = jnp.sum(wide_rows * wide_rows, axis=1)
        scaled = (wide_rows * gain[None, :]).astype(jnp.bfloat16)
        raw_logits = jnp.dot(scaled, weight, preferred_element_type=jnp.float32)
        inverse = lax.rsqrt(square_sum / full_width + norm_eps)
        normed = (scaled.astype(jnp.float32) * inverse[:, None]).astype(jnp.bfloat16)
        logits = raw_logits * inverse[:, None]
        choose = ids[:, :, None] == lax.iota(jnp.int32, experts)[None, None, :]
        picked = jnp.sum(jnp.where(choose, logits[:, None, :], 0.0), axis=-1)
        gate_probs = jax.nn.softmax(picked, axis=-1)
        onehot = choose.reshape(rows_dev * TOP, experts).astype(jnp.int32)
        earlier = jnp.cumsum(onehot, axis=0) - onehot
        slot_index = jnp.sum(earlier * onehot, axis=1).reshape(rows_dev, TOP)
        slot_key = ids * capacity + slot_index
        slot_hits = slot_key[None, :, :] == lax.iota(jnp.int32, experts * capacity)[:, None, None]
        route_matrix = jnp.any(slot_hits, axis=-1).astype(jnp.bfloat16)
        combine_matrix = jnp.sum(jnp.where(slot_hits, gate_probs[None, :, :], 0.0), axis=-1).T
        outgoing = jnp.dot(route_matrix, normed, preferred_element_type=jnp.float32).astype(
            jnp.bfloat16
        )
        outgoing = outgoing.reshape(n_ep, local_exp * capacity, full_width)
        incoming = lax.all_to_all(outgoing, "ep", split_axis=0, concat_axis=0, tiled=True)
        arrived = incoming.reshape(n_ep, local_exp, capacity, full_width).transpose(1, 0, 2, 3)
        arrived = arrived.reshape(local_exp, n_ep * capacity, full_width)
        gate_proj = jnp.einsum(
            "erd,edf->erf", arrived, w_gate[layer_idx], preferred_element_type=jnp.float32
        )
        up_proj = jnp.einsum(
            "erd,edf->erf", arrived, w_up[layer_idx], preferred_element_type=jnp.float32
        )
        inner = (jax.nn.silu(gate_proj) * up_proj).astype(jnp.bfloat16)
        down_local = w_down[layer_idx]

        def project():
            down_piece = lax.slice_in_dim(down_local, 0, local_width * lax.axis_size("tp"), axis=2)
            return jnp.einsum("erf,efd->der", inner, down_piece, preferred_element_type=jnp.float32)

        summed = lax.psum_scatter(
            project().astype(jnp.bfloat16), "tp", scatter_dimension=0, tiled=True
        ).astype(jnp.float32)
        out_rows = summed.astype(jnp.bfloat16).reshape(local_width, local_exp, n_ep, capacity)
        out_rows = out_rows.transpose(2, 1, 3, 0).reshape(n_ep, local_exp * capacity, local_width)
        returned = lax.all_to_all(out_rows, "ep", split_axis=0, concat_axis=0, tiled=True)
        returned = returned.reshape(experts * capacity, local_width).astype(jnp.float32)
        moe_out = jnp.dot(combine_matrix, returned, precision=lax.Precision.HIGHEST)
        current = (current.astype(jnp.float32) + moe_out).astype(jnp.bfloat16)
    return current


def solution(mesh):
    in_specs = (
        P("ep", "tp"),
        P(),
        P(),
        P(None, "ep", None, "tp"),
        P(None, "ep", None, "tp"),
        P(None, "ep", "tp", None),
        P(None, "ep", None),
    )
    out_specs = P("ep", "tp")
    return jax.shard_map(body, mesh=mesh, in_specs=in_specs, out_specs=out_specs, check_vma=False)
```

profile of v0, /device:TPU:0, one launch (start us, length us, event | category | flops | bytes accessed | tf_op | source)
XLA Modules:
  0.0 376.2 jit_solution(15348728780867839647)
XLA Ops:
  6.5 0.0 reduce-scatter.3.cloned.1.call-start
  6.5 0.7 fusion.79
  7.2 0.1 copy.38
  7.3 0.1 eq.102
  7.4 0.1 eq.98
  7.5 0.6 reduce-window.14
  8.1 0.2 slice_reduce_fusion.1
  8.3 0.1 fusion.69
  8.4 0.1 reshape.147
  8.5 0.2 fusion.41
  8.8 0.9 fusion.78
  9.6 15.9 %all_gather.6 = bf16[32,4096]{1,0:T(8,128)(2,1)S(1)} all-gather(bf16[32,1024]{1,0:T(8,128)(2,1)} %param.7), channel_id=1, replica_groups=mesh['ep'=8,'tp'=4] {'tp'}, dimensions={1}, use_global_device_ids=true | all-gather | bytes 327680 | tf_op jit(solution)/shard_map/all_gather | solution.py:26
  25.5 0.2 fusion.37
  25.7 1.3 convolution_convert_fusion.3
  27.0 0.0 slice-start
  27.0 52.8 %all_to_all.20 = bf16[8,64,4096]{2,1,0:T(8,128)(2,1)S(1)} all-to-all(bf16[8,64,4096]{2,1,0:T(8,128)(2,1)S(1)} %bitcast.120), channel_id=1, replica_groups=mesh['ep'=8,'tp'=4] {'ep'}, dimensions={0} | all-to-all | bytes 8388608 | tf_op jit(solution)/shard_map/all_to_all | solution.py:48
  79.8 0.5 copy.30
  80.3 0.0 copy-start
  80.3 2.0 copy-done
  82.3 0.0 slice-done
  82.3 0.0 slice-done.1
  82.3 1.5 fusion.10
  83.9 8.8 %fusion = bf16[4096,2,256]{0,2,1:T(8,128)(2,1)} fusion(bf16[2,2,192,4096]{3,2,1,0:T(8,128)(2,1)} %param.12, bf16[2,256,4096]{2,1,0:T(8,128)(2,1)} %bitcast.125, bf16[2,2,4096,192]{2,3,1,0:T(8,128)(2,1)} %param.11, f32[2,256,192]{1,2,0:T(8,128)S(1)} %fusion.10), kind=kOutput, calls=%fused_computation.4 | convolution fusion | flops 1613299712 | bytes 15073280 | tf_op jit(solution)/shard_map/erf,efd->der/dot_general | solution.py:62
  92.6 0.0 reduce-scatter.3.cloned.1.call-update
  92.7 0.1 copy.39
  92.8 0.1 eq.118
  92.8 0.1 eq.114
  92.9 0.6 reduce-window.16
  93.5 0.2 slice_reduce_fusion
  93.8 0.1 fusion.66
  93.9 0.1 reshape.155
  93.9 0.0 copy-done.3
  94.0 0.2 convolution_multiply_fusion.1
  94.1 75.1 %reduce-scatter.3.cloned.1.call-done = bf16[1024,2,256]{0,2,1:T(8,128)(2,1)} async-done(((bf16[4096,2,256]{0,2,1:T(8,128)(2,1)}), bf16[1024,2,256]{0,2,1:T(8,128)(2,1)}) %reduce-scatter.3.cloned.1.call-update) | async-done | bytes 1048592 | tf_op jit(solution)/shard_map/reduce_scatter | solution.py:64
  169.3 2.3 copy.31
  171.6 3.6 all-to-all-start.1
  175.2 0.0 reduce-scatter.5.cloned.1.call-start
  175.4 0.1 copy.29
  175.4 0.2 fusion.40
  175.7 0.2 select_reduce_fusion.1
  175.9 14.7 %all-to-all-done.1 = bf16[8,64,1024]{2,1,0:T(8,128)(2,1)S(1)} async-done(((bf16[8,64,1024]{2,1,0:T(8,128)(2,1)}), bf16[8,64,1024]{2,1,0:T(8,128)(2,1)S(1)}, u32[]{:S(2)}, u32[]{:S(2)}) %all-to-all-start.1) | async-done | bytes 1048608 | tf_op jit(solution)/shard_map/all_to_all | solution.py:69
  190.6 0.0 copy-done.2
  190.6 0.6 fusion.30
  191.2 14.4 %all_gather.7 = bf16[32,4096]{1,0:T(8,128)(2,1)S(1)} all-gather(bf16[32,1024]{1,0:T(8,128)(2,1)S(1)} %fusion.30), channel_id=1, replica_groups=mesh['ep'=8,'tp'=4] {'tp'}, dimensions={1}, use_global_device_ids=true | all-gather | bytes 327680 | tf_op jit(solution)/shard_map/all_gather | solution.py:26
  205.6 0.2 fusion.39
  205.8 1.3 convolution_convert_fusion.1
  207.1 0.0 slice-start.2
  207.1 51.8 %all_to_all.21 = bf16[8,64,4096]{2,1,0:T(8,128)(2,1)S(1)} all-to-all(bf16[8,64,4096]{2,1,0:T(8,128)(2,1)S(1)} %bitcast.122), channel_id=1, replica_groups=mesh['ep'=8,'tp'=4] {'ep'}, dimensions={0} | all-to-all | bytes 8388608 | tf_op jit(solution)/shard_map/all_to_all | solution.py:48
  258.9 0.5 copy.36
  259.4 0.0 copy-start.1
  259.4 2.0 copy-done.1
  261.4 0.0 slice-done.2
  261.4 0.0 slice-done.3
  261.4 1.5 fusion.5
  262.9 8.8 %fusion.1 = bf16[4096,2,256]{0,2,1:T(8,128)(2,1)} fusion(bf16[2,2,192,4096]{3,2,1,0:T(8,128)(2,1)} %param.12, bf16[2,256,4096]{2,1,0:T(8,128)(2,1)} %bitcast.127, bf16[2,2,4096,192]{2,3,1,0:T(8,128)(2,1)} %param.11, f32[2,256,192]{1,2,0:T(8,128)S(1)} %fusion.5), kind=kOutput, calls=%fused_computation.5 | convolution fusion | flops 1613299712 | bytes 15073280 | tf_op jit(solution)/shard_map/erf,efd->der/dot_general | solution.py:62
  271.7 0.0 reduce-scatter.5.cloned.1.call-update
  271.7 75.0 %reduce-scatter.5.cloned.1.call-done = bf16[1024,2,256]{0,2,1:T(8,128)(2,1)} async-done(((bf16[4096,2,256]{0,2,1:T(8,128)(2,1)}), bf16[1024,2,256]{0,2,1:T(8,128)(2,1)}) %reduce-scatter.5.cloned.1.call-update) | async-done | bytes 1048592 | tf_op jit(solution)/shard_map/reduce_scatter | solution.py:64
  346.7 2.3 copy.37
  349.0 3.7 all-to-all-start.3
  352.7 0.2 convolution_multiply_fusion
  353.0 0.1 copy.35
  353.1 0.2 select_reduce_fusion
  353.3 14.8 %all-to-all-done.3 = bf16[8,64,1024]{2,1,0:T(8,128)(2,1)S(1)} async-done(((bf16[8,64,1024]{2,1,0:T(8,128)(2,1)}), bf16[8,64,1024]{2,1,0:T(8,128)(2,1)S(1)}, u32[]{:S(2)}, u32[]{:S(2)}) %all-to-all-start.3) | async-done | bytes 1048608 | tf_op jit(solution)/shard_map/all_to_all | solution.py:69
  368.1 1.2 fusion.31
  (24 shorter events, 0.3 us)
Async XLA Ops:
  6.5 162.8 %reduce-scatter.3.cloned.1.call-start = ((), (), s32[]{:S(2)}) async-start(), calls=%async_computation.6 | async-start | bytes 5242880 | tf_op jit(solution)/shard_map/reduce_scatter | solution.py:64
  27.0 55.3 %slice-start = ((s8[6291456]{0:T(1024)(128)(4,1)}), s8[4194304]{0:T(1024)(128)(4,1)S(1)}, s32[]{:S(2)}) async-start(s8[6291456]{0:T(1024)(128)(4,1)} %bitcast.136), calls=%async_computation.8 | async-start | bytes 8388608
  79.8 2.5 slice-start.1
  80.3 2.0 copy-start
  92.6 1.3 copy-start.3
  92.6 98.0 %copy-start.2 = (bf16[32,1024]{1,0:T(8,128)(2,1)S(1)}, bf16[32,1024]{1,0:T(8,128)(2,1)}, u32[]{:S(2)}) copy-start(bf16[32,1024]{1,0:T(8,128)(2,1)} %param.7) | copy-start | bytes 196612
  171.6 19.0 %all-to-all-start.1 = ((bf16[8,64,1024]{2,1,0:T(8,128)(2,1)}), bf16[8,64,1024]{2,1,0:T(8,128)(2,1)S(1)}, u32[]{:S(2)}, u32[]{:S(2)}) async-start(bf16[8,64,1024]{2,1,0:T(8,128)(2,1)} %bitcast.16), calls=%async_computation.2 | async-start | bytes 2097152 | tf_op jit(solution)/shard_map/all_to_all | solution.py:69
  175.2 171.5 %reduce-scatter.5.cloned.1.call-start = ((), (), s32[]{:S(2)}) async-start(), calls=%async_computation.7 | async-start | bytes 5242880 | tf_op jit(solution)/shard_map/reduce_scatter | solution.py:64
  207.1 54.3 %slice-start.2 = ((s8[6291456]{0:T(1024)(128)(4,1)}), s8[4194304]{0:T(1024)(128)(4,1)S(1)}, s32[]{:S(2)}) async-start(s8[6291456]{0:T(1024)(128)(4,1)} %bitcast.138), calls=%async_computation.10 | async-start | bytes 8388608
  258.9 2.5 slice-start.3
  259.4 2.0 copy-start.1
  349.0 19.0 %all-to-all-start.3 = ((bf16[8,64,1024]{2,1,0:T(8,128)(2,1)}), bf16[8,64,1024]{2,1,0:T(8,128)(2,1)S(1)}, u32[]{:S(2)}, u32[]{:S(2)}) async-start(bf16[8,64,1024]{2,1,0:T(8,128)(2,1)} %bitcast.34), calls=%async_computation.5 | async-start | bytes 2097152 | tf_op jit(solution)/shard_map/all_to_all | solution.py:69
Sparse Core Ops, SparseCore 0:
  92.8 76.4 reduce-scatter.2
  271.8 74.8 reduce-scatter.4
where the time goes:
time: 377 us; the launch traced here: 376 us
  waiting for transfers between devices  180 us (48%)
  blocking collectives  135 us (36%)
  matrix products  25.5 us (7%)
  between operations  13.6 us (4%)
  local copies, waits for them, and re-layouts  12.3 us (3%)
  starting transfers between devices  7.32 us (2%)
    reduce_scatter x2, waiting for transfers between devices, body(): lax.psum_scatter(project().astype(jnp.bfloat16), 'tp', scatter_dimension=...  150 us
    all_to_all x2, blocking collectives, body(): lax.all_to_all(outgoing, 'ep', split_axis=0, concat_axis=0, tiled=True)  105 us
    all_gather x2, blocking collectives, body(): whole = lax.all_gather(current, 'tp', axis=1, tiled=True)  30.2 us
    all_to_all x2, waiting for transfers between devices, body(): lax.all_to_all(out_rows, 'ep', split_axis=0, concat_axis=0, tiled=True)  29.5 us
    dot_general x2, matrix products, project(): jnp.einsum('erf,efd->der', inner, down_piece, preferred_element_type=jnp....  17.6 us
  transfers between devices with their start and end apart: 4, of which 4 were waited for; matrix products, arithmetic and copies ran while one was open for 1% of the time, Pallas kernels for 0%

commit v1 on v0

--- a/solution.py
+++ b/solution.py
@@ -6,6 +6,16 @@
 TOP = 8
 LAYERS = 2
 norm_eps = 1e-06
+
+
+def gather_by_hops(x, mesh_axis, dim):
+    n_dev = lax.axis_size(mesh_axis)
+    held, blocks = (x, [x])
+    for _ in range(n_dev - 1):
+        held = lax.ppermute(held, mesh_axis, [(i, (i + 1) % n_dev) for i in range(n_dev)])
+        blocks.insert(0, held)
+    row_of_blocks = jnp.concatenate(blocks, axis=dim)
+    return jnp.roll(row_of_blocks, (lax.axis_index(mesh_axis) + 1) * x.shape[dim], axis=dim)
 
 
 def body(tokens, norm_gains, router, w_gate, w_up, w_down, expert_ids):
@@ -23,7 +33,7 @@
         weight = router[layer_idx]
         ids = expert_ids[layer_idx]
         normed = None
-        whole = lax.all_gather(current, "tp", axis=1, tiled=True)
+        whole = gather_by_hops(current, "tp", 1)
         wide_rows = whole.astype(jnp.float32)
         square_sum = jnp.sum(wide_rows * wide_rows, axis=1)
         scaled = (wide_rows * gain[None, :]).astype(jnp.bfloat16)

time: 377 us -> 379 us (level)
  blocking collectives: 135 us -> 105 us
  waiting for transfers between devices: 180 us -> 205 us
  starting transfers between devices: 7.32 us -> 12.2 us
    all_gather x2 -> x0, blocking collectives: 30.2 us -> none  [body(): whole = lax.all_gather(current, 'tp', axis=1, tiled=True)]
    ppermute x0 -> x6, waiting for transfers between devices: none -> 30.2 us  [gather_by_hops(): lax.ppermute(held, mesh_axis, [(i, (i + 1) % n_dev) for i in range(n_dev)])]
    ppermute x0 -> x6, starting transfers between devices: none -> 4.81 us  [gather_by_hops(): lax.ppermute(held, mesh_axis, [(i, (i + 1) % n_dev) for i in range(n_dev)])]
    reduce_scatter x2, waiting for transfers between devices: 150 us -> 146 us  [body(): lax.psum_scatter(project().astype(jnp.bfloat16), 'tp', scatter_dimension=...]
  transfers between devices with their start and end apart: 4 -> 10, of which waited for: 4 -> 10; matrix products, arithmetic and copies ran while one was open for 1% -> 2% of each run, Pallas kernels for 0% -> 0%
where the time goes in v1:
time: 379 us
  waiting for transfers between devices  205 us (54%)
  blocking collectives  105 us (28%)
  matrix products  25.5 us (7%)
  between operations  13.6 us (4%)
  local copies, waits for them, and re-layouts  12.3 us (3%)
  starting transfers between devices  12.2 us (3%)
  other arithmetic  5.04 us (1%)
    reduce_scatter x2, waiting for transfers between devices, body(): lax.psum_scatter(project().astype(jnp.bfloat16), 'tp', scatter_dimension=...  146 us
    all_to_all x2, blocking collectives, body(): lax.all_to_all(outgoing, 'ep', split_axis=0, concat_axis=0, tiled=True)  105 us
    ppermute x6, waiting for transfers between devices, gather_by_hops(): lax.ppermute(held, mesh_axis, [(i, (i + 1) % n_dev) for i in range(n_dev)])  30.2 us
    all_to_all x2, waiting for transfers between devices, body(): lax.all_to_all(out_rows, 'ep', split_axis=0, concat_axis=0, tiled=True)  29.3 us
    dot_general x2, matrix products, project(): jnp.einsum('erf,efd->der', inner, down_piece, preferred_element_type=jnp....  17.6 us
  transfers between devices with their start and end apart: 10, of which 10 were waited for; matrix products, arithmetic and copies ran while one was open for 2% of the time, Pallas kernels for 0%

profile of v1, /device:TPU:0, one launch (start us, length us, event | category | flops | bytes accessed | tf_op | source)
XLA Modules:
  0.0 378.6 jit_solution(17621679789536355626)
XLA Ops:
  6.5 3.1 collective-permute-start
  9.6 0.7 fusion.95
  10.3 0.1 copy.38
  10.4 0.1 eq.104
  10.5 0.1 eq.100
  10.6 0.6 reduce-window.14
  11.2 0.2 slice_reduce_fusion.1
  11.4 0.9 fusion.94
  12.3 0.1 fusion.83
  12.3 0.1 reshape.147
  12.4 1.6 collective-permute-done
  14.1 0.0 collective-permute-start.1
  14.1 6.0 %collective-permute-done.1 = bf16[32,1024]{1,0:T(8,128)(2,1)S(1)} collective-permute-done((bf16[32,1024]{1,0:T(8,128)(2,1)S(1)}, bf16[32,1024]{1,0:T(8,128)(2,1)S(1)}, u32[]{:S(2)}, u32[]{:S(2)}) %collective-permute-start.1) | collective-permute-done | bytes 65568 | tf_op jit(solution)/shard_map/ppermute | solution.py:15
  20.1 0.2 fusion.41
  20.4 5.8 %collective-permute-done.2 = bf16[32,1024]{1,0:T(8,128)(2,1)S(1)} collective-permute-done((bf16[32,1024]{1,0:T(8,128)(2,1)S(1)}, bf16[32,1024]{1,0:T(8,128)(2,1)S(1)}, u32[]{:S(2)}, u32[]{:S(2)}) %collective-permute-start.2) | collective-permute-done | bytes 65568 | tf_op jit(solution)/shard_map/ppermute | solution.py:15
  26.2 1.6 fusion.37
  27.8 1.3 convolution_convert_fusion.3
  29.1 0.0 slice-start
  29.1 53.0 %all_to_all.20 = bf16[8,64,4096]{2,1,0:T(8,128)(2,1)S(1)} all-to-all(bf16[8,64,4096]{2,1,0:T(8,128)(2,1)S(1)} %bitcast.120), channel_id=1, replica_groups=mesh['ep'=8,'tp'=4] {'ep'}, dimensions={0} | all-to-all | bytes 8388608 | tf_op jit(solution)/shard_map/all_to_all | solution.py:58
  82.2 0.5 copy.30
  82.7 2.0 copy-done
  84.6 1.5 fusion.10
  86.2 8.8 %fusion = bf16[4096,2,256]{0,2,1:T(8,128)(2,1)} fusion(bf16[2,2,192,4096]{3,2,1,0:T(8,128)(2,1)} %param.14, bf16[2,256,4096]{2,1,0:T(8,128)(2,1)} %bitcast.125, bf16[2,2,4096,192]{2,3,1,0:T(8,128)(2,1)} %param.13, f32[2,256,192]{1,2,0:T(8,128)S(1)} %fusion.10), kind=kOutput, calls=%fused_computation.4 | convolution fusion | flops 1613299712 | bytes 15073280 | tf_op jit(solution)/shard_map/erf,efd->der/dot_general | solution.py:72
  95.0 0.0 reduce-scatter.3.cloned.1.call-update
  95.0 0.1 copy.39
  95.1 0.1 eq.120
  95.1 0.1 eq.116
  95.3 0.6 reduce-window.16
  95.8 72.4 %reduce-scatter.3.cloned.1.call-done = bf16[1024,2,256]{0,2,1:T(8,128)(2,1)} async-done(((bf16[4096,2,256]{0,2,1:T(8,128)(2,1)}), bf16[1024,2,256]{0,2,1:T(8,128)(2,1)}) %reduce-scatter.3.cloned.1.call-update) | async-done | bytes 1048592 | tf_op jit(solution)/shard_map/reduce_scatter | solution.py:74
  168.3 2.3 copy.31
  170.6 3.7 all-to-all-start.1
  174.2 0.0 reduce-scatter.5.cloned.1.call-start
  174.3 0.2 slice_reduce_fusion
  174.5 0.2 convolution_multiply_fusion.1
  174.8 0.1 copy.29
  174.9 0.2 select_reduce_fusion.1
  175.1 14.5 %all-to-all-done.1 = bf16[8,64,1024]{2,1,0:T(8,128)(2,1)S(1)} async-done(((bf16[8,64,1024]{2,1,0:T(8,128)(2,1)}), bf16[8,64,1024]{2,1,0:T(8,128)(2,1)S(1)}, u32[]{:S(2)}, u32[]{:S(2)}) %all-to-all-start.1) | async-done | bytes 1048608 | tf_op jit(solution)/shard_map/all_to_all | solution.py:79
  189.6 0.6 fusion.30
  190.2 1.5 collective-permute-start.3
  191.8 0.1 fusion.80
  191.8 0.1 reshape.155
  191.9 4.4 %collective-permute-done.3 = bf16[32,1024]{1,0:T(8,128)(2,1)S(1)} collective-permute-done((bf16[32,1024]{1,0:T(8,128)(2,1)S(1)}, bf16[32,1024]{1,0:T(8,128)(2,1)S(1)}, u32[]{:S(2)}, u32[]{:S(2)}) %collective-permute-start.3) | collective-permute-done | bytes 65568 | tf_op jit(solution)/shard_map/ppermute | solution.py:15
  196.3 0.2 collective-permute-start.4
  196.6 6.4 %collective-permute-done.4 = bf16[32,1024]{1,0:T(8,128)(2,1)S(1)} collective-permute-done((bf16[32,1024]{1,0:T(8,128)(2,1)S(1)}, bf16[32,1024]{1,0:T(8,128)(2,1)S(1)}, u32[]{:S(2)}, u32[]{:S(2)}) %collective-permute-start.4) | collective-permute-done | bytes 65568 | tf_op jit(solution)/shard_map/ppermute | solution.py:15
  203.0 0.0 collective-permute-start.5
  203.0 0.2 fusion.40
  203.2 5.8 %collective-permute-done.5 = bf16[32,1024]{1,0:T(8,128)(2,1)S(1)} collective-permute-done((bf16[32,1024]{1,0:T(8,128)(2,1)S(1)}, bf16[32,1024]{1,0:T(8,128)(2,1)S(1)}, u32[]{:S(2)}, u32[]{:S(2)}) %collective-permute-start.5) | collective-permute-done | bytes 65568 | tf_op jit(solution)/shard_map/ppermute | solution.py:15
  209.0 0.9 fusion.39
  210.0 1.3 convolution_convert_fusion.1
  211.3 0.0 slice-start.2
  211.3 51.8 %all_to_all.21 = bf16[8,64,4096]{2,1,0:T(8,128)(2,1)S(1)} all-to-all(bf16[8,64,4096]{2,1,0:T(8,128)(2,1)S(1)} %bitcast.122), channel_id=1, replica_groups=mesh['ep'=8,'tp'=4] {'ep'}, dimensions={0} | all-to-all | bytes 8388608 | tf_op jit(solution)/shard_map/all_to_all | solution.py:58
  263.1 0.5 copy.36
  263.6 2.0 copy-done.1
  265.6 1.5 fusion.5
  267.1 8.8 %fusion.1 = bf16[4096,2,256]{0,2,1:T(8,128)(2,1)} fusion(bf16[2,2,192,4096]{3,2,1,0:T(8,128)(2,1)} %param.14, bf16[2,256,4096]{2,1,0:T(8,128)(2,1)} %bitcast.127, bf16[2,2,4096,192]{2,3,1,0:T(8,128)(2,1)} %param.13, f32[2,256,192]{1,2,0:T(8,128)S(1)} %fusion.5), kind=kOutput, calls=%fused_computation.5 | convolution fusion | flops 1613299712 | bytes 15073280 | tf_op jit(solution)/shard_map/erf,efd->der/dot_general | solution.py:72
  275.9 0.0 reduce-scatter.5.cloned.1.call-update
  275.9 73.3 %reduce-scatter.5.cloned.1.call-done = bf16[1024,2,256]{0,2,1:T(8,128)(2,1)} async-done(((bf16[4096,2,256]{0,2,1:T(8,128)(2,1)}), bf16[1024,2,256]{0,2,1:T(8,128)(2,1)}) %reduce-scatter.5.cloned.1.call-update) | async-done | bytes 1048592 | tf_op jit(solution)/shard_map/reduce_scatter | solution.py:74
  349.2 2.3 copy.37
  351.5 3.7 all-to-all-start.3
  355.2 0.2 convolution_multiply_fusion
  355.4 0.1 copy.35
  355.5 0.2 select_reduce_fusion
  355.7 14.8 %all-to-all-done.3 = bf16[8,64,1024]{2,1,0:T(8,128)(2,1)S(1)} async-done(((bf16[8,64,1024]{2,1,0:T(8,128)(2,1)}), bf16[8,64,1024]{2,1,0:T(8,128)(2,1)S(1)}, u32[]{:S(2)}, u32[]{:S(2)}) %all-to-all-start.3) | async-done | bytes 1048608 | tf_op jit(solution)/shard_map/all_to_all | solution.py:79
  370.5 1.2 fusion.31
  (34 shorter events, 0.3 us)
Async XLA Ops:
  6.5 161.7 %reduce-scatter.3.cloned.1.call-start = ((), (), s32[]{:S(2)}) async-start(), calls=%async_computation.6 | async-start | bytes 5242880 | tf_op jit(solution)/shard_map/reduce_scatter | solution.py:74
  6.5 7.5 %collective-permute-start = (bf16[32,1024]{1,0:T(8,128)(2,1)}, bf16[32,1024]{1,0:T(8,128)(2,1)S(1)}, u32[]{:S(2)}, u32[]{:S(2)}) collective-permute-start(bf16[32,1024]{1,0:T(8,128)(2,1)} %param.9), channel_id=1, source_target_pairs={{0,1},{1,2},{2,3},{3,0},{4,5},{5,6},{6,7},{7,4},{8,9},{9,10},{10,1... | collective-permute-start | bytes 196616 | tf_op jit(solution)/shard_map/ppermute | solution.py:15
  14.1 6.1 %collective-permute-start.1 = (bf16[32,1024]{1,0:T(8,128)(2,1)S(1)}, bf16[32,1024]{1,0:T(8,128)(2,1)S(1)}, u32[]{:S(2)}, u32[]{:S(2)}) collective-permute-start(bf16[32,1024]{1,0:T(8,128)(2,1)S(1)} %collective-permute-done), channel_id=1, source_target_pairs={{0,1},{1,2},{2,3},{3,0},{4,5},{5,6},{6,7},{7,4},{8,9},{9,10},{10,1... | collective-permute-start | bytes 196616 | tf_op jit(solution)/shard_map/ppermute | solution.py:15
  20.1 6.1 %collective-permute-start.2 = (bf16[32,1024]{1,0:T(8,128)(2,1)S(1)}, bf16[32,1024]{1,0:T(8,128)(2,1)S(1)}, u32[]{:S(2)}, u32[]{:S(2)}) collective-permute-start(bf16[32,1024]{1,0:T(8,128)(2,1)S(1)} %collective-permute-done.1), channel_id=1, source_target_pairs={{0,1},{1,2},{2,3},{3,0},{4,5},{5,6},{6,7},{7,4},{8,9},{9,10},{10,1... | collective-permute-start | bytes 196616 | tf_op jit(solution)/shard_map/ppermute | solution.py:15
  29.1 55.5 %slice-start = ((s8[6291456]{0:T(1024)(128)(4,1)}), s8[4194304]{0:T(1024)(128)(4,1)S(1)}, s32[]{:S(2)}) async-start(s8[6291456]{0:T(1024)(128)(4,1)} %bitcast.136), calls=%async_computation.8 | async-start | bytes 8388608
  82.2 2.5 slice-start.1
  82.6 2.0 copy-start
  95.0 79.6 %copy-start.3 = (bf16[2,4096,16]{1,2,0:T(8,128)(2,1)S(1)}, bf16[2,4096,16]{1,2,0:T(8,128)(2,1)}, u32[]{:S(2)}) copy-start(bf16[2,4096,16]{1,2,0:T(8,128)(2,1)} %param.11) | copy-start | bytes 786436
  95.0 94.7 %copy-start.2 = (bf16[32,1024]{1,0:T(8,128)(2,1)S(1)}, bf16[32,1024]{1,0:T(8,128)(2,1)}, u32[]{:S(2)}) copy-start(bf16[32,1024]{1,0:T(8,128)(2,1)} %param.9) | copy-start | bytes 196612
  170.6 19.0 %all-to-all-start.1 = ((bf16[8,64,1024]{2,1,0:T(8,128)(2,1)}), bf16[8,64,1024]{2,1,0:T(8,128)(2,1)S(1)}, u32[]{:S(2)}, u32[]{:S(2)}) async-start(bf16[8,64,1024]{2,1,0:T(8,128)(2,1)} %bitcast.16), calls=%async_computation.2 | async-start | bytes 2097152 | tf_op jit(solution)/shard_map/all_to_all | solution.py:79
  174.2 175.0 %reduce-scatter.5.cloned.1.call-start = ((), (), s32[]{:S(2)}) async-start(), calls=%async_computation.7 | async-start | bytes 5242880 | tf_op jit(solution)/shard_map/reduce_scatter | solution.py:74
  190.2 6.1 %collective-permute-start.3 = (bf16[32,1024]{1,0:T(8,128)(2,1)S(1)}, bf16[32,1024]{1,0:T(8,128)(2,1)S(1)}, u32[]{:S(2)}, u32[]{:S(2)}) collective-permute-start(bf16[32,1024]{1,0:T(8,128)(2,1)S(1)} %fusion.30), channel_id=1, source_target_pairs={{0,1},{1,2},{2,3},{3,0},{4,5},{5,6},{6,7},{7,4},{8,9},{9,10},{10,1... | collective-permute-start | bytes 196616 | tf_op jit(solution)/shard_map/ppermute | solution.py:15
  196.3 6.6 %collective-permute-start.4 = (bf16[32,1024]{1,0:T(8,128)(2,1)S(1)}, bf16[32,1024]{1,0:T(8,128)(2,1)S(1)}, u32[]{:S(2)}, u32[]{:S(2)}) collective-permute-start(bf16[32,1024]{1,0:T(8,128)(2,1)S(1)} %collective-permute-done.3), channel_id=1, source_target_pairs={{0,1},{1,2},{2,3},{3,0},{4,5},{5,6},{6,7},{7,4},{8,9},{9,10},{10,1... | collective-permute-start | bytes 196616 | tf_op jit(solution)/shard_map/ppermute | solution.py:15
  203.0 6.1 %collective-permute-start.5 = (bf16[32,1024]{1,0:T(8,128)(2,1)S(1)}, bf16[32,1024]{1,0:T(8,128)(2,1)S(1)}, u32[]{:S(2)}, u32[]{:S(2)}) collective-permute-start(bf16[32,1024]{1,0:T(8,128)(2,1)S(1)} %collective-permute-done.4), channel_id=1, source_target_pairs={{0,1},{1,2},{2,3},{3,0},{4,5},{5,6},{6,7},{7,4},{8,9},{9,10},{10,1... | collective-permute-start | bytes 196616 | tf_op jit(solution)/shard_map/ppermute | solution.py:15
  211.3 54.3 %slice-start.2 = ((s8[6291456]{0:T(1024)(128)(4,1)}), s8[4194304]{0:T(1024)(128)(4,1)S(1)}, s32[]{:S(2)}) async-start(s8[6291456]{0:T(1024)(128)(4,1)} %bitcast.138), calls=%async_computation.10 | async-start | bytes 8388608
  263.1 2.5 slice-start.3
  263.6 2.0 copy-start.1
  351.5 19.0 %all-to-all-start.3 = ((bf16[8,64,1024]{2,1,0:T(8,128)(2,1)}), bf16[8,64,1024]{2,1,0:T(8,128)(2,1)S(1)}, u32[]{:S(2)}, u32[]{:S(2)}) async-start(bf16[8,64,1024]{2,1,0:T(8,128)(2,1)} %bitcast.34), calls=%async_computation.5 | async-start | bytes 2097152 | tf_op jit(solution)/shard_map/all_to_all | solution.py:79
Sparse Core Ops, SparseCore 0:
  95.1 73.1 reduce-scatter.2
  276.1 73.0 reduce-scatter.4
